TPU v7x, 32 devices: a whole 2x2x4 slice. The times are simulated.
32 devices in a mesh: dp: 4 (over x, core), section: 2 (over y), mp: 4 (over z).
Axes of the slice: x: 2, y: 2, z: 4, core: 2. Of those that a mesh axis runs over, the one named last changes fastest.
Arguments:
- micro_inputs: bfloat16 [8, 64, 4096], P(('dp', 'section'), None, 'mp'), parts along dimension 0, may hold values from -6 to 6
- qkv_weight: bfloat16 [2, 4096, 3, 2048], P('section', None, None, 'mp'), may hold values from -0.09375 to 0.09375
- out_weight: bfloat16 [2, 2048, 4096], P('section', None, 'mp'), may hold values from -0.125 to 0.125
- norm_gain: bfloat16 [2, 4096], P('section'), may hold values from 0.099609375 to 1.8984375
- position_bias: float32 [32, 32], P('mp'), may hold values from -3 to 280
Outputs:
- encoded: bfloat16 [8, 64, 4096], P(('dp', 'section'), None, 'mp'), parts along dimension 0
There are 4 independent parts, one for each index of `dp`. A program takes and returns all parts, laid end to end along the dimension named above; an argument that names none is the same for every part. Nothing has to cross between parts.
All inputs are finite; a program needn't handle non-finite values.
Results may differ from a plain program's by a relative error of at most 0.025.
Values may be sent and summed in bfloat16 or wider, within the bound.
No kernel may reach another device: no remote copies, remote signals or barrier semaphores. Data moves between devices by JAX's collectives and lax.ppermute only.
A program may use at most 128 MiB of HBM per device.

v0:
```python
import math

import jax
import jax.numpy as jnp
import numpy as np
from jax import lax
from jax.experimental import pallas as pl
from jax.experimental.pallas import tpu as pltpu
from jax.sharding import PartitionSpec as P


REACH = 128
NORM_EPSILON = 0.1
MOST_DIRECT = 4
FIRST_ORDER = (3, 1, 2)
MIX_ORDER = (2, 3, 1)
REST_ORDER = (3, 1)
FAR = 2
LANES = 128
F32 = jnp.float32
BF16 = jnp.bfloat16
VMEM = pltpu.VMEM


def bucket_table(length, bucket_count, reach_limit):
    offset = np.arange(length)[None, :] - np.arange(length)[:, None]
    half_count = bucket_count // 2
    upper_side = (offset > 0).astype(np.int32) * half_count
    distance = np.abs(offset)
    exact_count = half_count // 2
    scaled = (
        np.log(np.maximum(distance, 1) / exact_count)
        / np.log(reach_limit / exact_count)
        * (half_count - exact_count)
    )
    far_bucket = np.minimum(exact_count + scaled.astype(np.int32), half_count - 1)
    return (upper_side + np.where(distance < exact_count, distance, far_bucket)).astype(np.int32)


def swap_masks(peers, order=MIX_ORDER):
    if peers & (peers - 1) or peers > MOST_DIRECT:
        return None
    return [mask for mask in order if mask < peers]


def permuted(x, target):
    sections, peers = lax.axis_size("section"), lax.axis_size("mp")
    pairs = []
    for s in range(sections):
        for i in range(peers):
            to_section, to_place = target(s, i)
            pairs.append((s * peers + i, to_section * peers + to_place))
    return lax.ppermute(x, ("section", "mp"), pairs)


def swapped(x, mask, section=None):
    return permuted(x, lambda s, i: (s, i ^ (mask if section in (None, s) else 1)))


def crossed(x, mask, section):
    return permuted(x, lambda s, i: (s ^ 1, i ^ mask if s == section else i))


def from_peers(x, order=MIX_ORDER, section=None):
    masks = swap_masks(lax.axis_size("mp"), order)
    if masks is None:
        return [(None, (lax.all_gather(x, "mp", axis=0, tiled=False),))]
    return [(mask, (swapped(x, mask, section),)) for mask in masks]


def chosen(refs):
    if len(refs) == 1:
        return refs[0][...]
    return jnp.where(lax.axis_index("section") == 0, refs[0][...], refs[1][...])


def peer_blocks(masks, groups):
    peers = lax.axis_size("mp")
    me = lax.axis_index("mp")
    if masks == [None]:
        turned = [lax.rem(me + step, peers) for step in range(1, peers)]
        return [(peer, groups[0][0][peer]) for peer in turned]
    return [(me ^ mask, chosen(refs)) for mask, refs in zip(masks, groups)]


def grouped(refs, sizes):
    groups = []
    for size in sizes:
        groups.append(refs[:size])
        refs = refs[size:]
    return groups, refs


def rows_of(peer, count):
    return pl.ds(pl.multiple_of(peer * count, count), count)


def call(body, outs, *args, specs=None, scratch=(), limit=8):
    specs = specs or [pl.BlockSpec(memory_space=VMEM)] * len(args)
    run = pl.pallas_call(
        body,
        in_specs=specs,
        out_specs=tuple(pl.BlockSpec(memory_space=VMEM) for _ in outs),
        out_shape=tuple(outs),
        scratch_shapes=list(scratch),
        compiler_params=pltpu.CompilerParams(vmem_limit_bytes=limit << 20),
    )
    return run(*args)


def add_part(peer, block, gain_ref, weight_ref, total_ref, squares):
    width = block.shape[1]
    rows = block.astype(F32)
    gain = gain_ref[:, rows_of(peer, width)].astype(F32)
    gained = (rows * gain).astype(BF16)
    for lane in range(0, width, LANES):
        tile = rows[:, lane : lane + LANES]
        squares = squares + tile * tile
    for kind in range(weight_ref.shape[0]):
        part = weight_ref[kind, rows_of(peer, width), :]
        total_ref[kind] += jnp.dot(gained, part, preferred_element_type=F32)
    return squares


def own_part(peer, block, gain_ref, weight_ref, total_ref, squares_ref):
    total_ref[...] = jnp.zeros_like(total_ref)
    squares = jnp.zeros(squares_ref.shape, F32)
    squares_ref[...] = add_part(peer, block, gain_ref, weight_ref, total_ref, squares)


def load_kernel(x_in, gain_in, qkv_in, table_ref, grid_in,
                x_ref, gain_ref, held_qkv, total_ref, squares_ref, bias_ref,
                grid_ref, sems):
    peers = lax.axis_size("mp")
    me = lax.axis_index("mp")
    width = x_in.shape[1]
    pairs = [(grid_in, grid_ref), (x_in, x_ref), (gain_in, gain_ref)]
    for step in range(peers):
        rows = rows_of(lax.rem(me + step, peers), width)
        pairs.append((qkv_in.at[:, rows, :], held_qkv.at[:, rows, :]))
    copies = [pltpu.make_async_copy(a, b, sems.at[i]) for i, (a, b) in enumerate(pairs)]
    for copy in copies:
        copy.start()
    heads, buckets = table_ref.shape
    length = grid_ref.shape[0]
    copies[0].wait()

    def one_head(head, carry):
        grid = grid_ref[...]
        bias = jnp.zeros(grid.shape, F32)
        for bucket in range(buckets):
            bias = jnp.where(grid == bucket, table_ref[head, bucket], bias)
        bias_ref[rows_of(head, length), :] = bias
        return carry

    lax.fori_loop(0, heads, one_head, 0)
    for copy in copies[1:4]:
        copy.wait()
    own_part(me, x_ref[...], gain_ref, held_qkv, total_ref, squares_ref)
    for copy in copies[4:]:
        copy.wait()


def fetch_kernel(whole_in, held_ref, sems):
    count = sems.shape[0]
    rows = whole_in.shape[0] // count
    copies = [
        pltpu.make_async_copy(
            whole_in.at[pl.ds(part * rows, rows), :],
            held_ref.at[pl.ds(part * rows, rows), :],
            sems.at[part],
        )
        for part in range(count)
    ]
    for copy in copies:
        copy.start()
    for copy in copies:
        copy.wait()


def own_kernel(*refs):
    *block_refs, gain_ref, held_qkv, stream_ref, total_ref, squares_ref = refs
    block = chosen(block_refs)
    stream_ref[...] = block
    own_part(lax.axis_index("mp"), block, gain_ref, held_qkv, total_ref, squares_ref)


def add_kernel(masks, sizes, *refs):
    peer_refs, rest = grouped(refs, sizes)
    gain_ref, held_qkv, partial_ref, partial_squares, total_ref, squares_ref = rest
    total_ref[...] = partial_ref[...]
    squares = partial_squares[...]
    for peer, block in peer_blocks(masks, peer_refs):
        squares = add_part(peer, block, gain_ref, held_qkv, total_ref, squares)
    squares_ref[...] = squares


def attend_kernel(masks, sizes, head_size, model_width, *refs):
    peer_refs, rest = grouped(refs, sizes)
    gain_ref, held_qkv, partial_ref, partial_squares, bias_ref, mix_ref, total_ref = rest
    total_ref[...] = partial_ref[...]
    squares = partial_squares[...]
    for peer, block in peer_blocks(masks, peer_refs):
        squares = add_part(peer, block, gain_ref, held_qkv, total_ref, squares)
    mean_square = jnp.sum(squares, axis=1, keepdims=True) / model_width
    row_scale = lax.rsqrt(mean_square + NORM_EPSILON)
    length, local_qkv = mix_ref.shape
    score_scale = 1.0 / math.sqrt(head_size)
    block_heads = LANES // head_size
    lane = lax.broadcasted_iota(jnp.int32, (length, LANES), 1) // head_size
    for block in range(local_qkv // LANES):
        lanes = pl.ds(block * LANES, LANES)
        queries, keys, values = (total_ref[kind, :, lanes] * row_scale for kind in range(3))
        keys = keys.astype(BF16)
        values = values.astype(BF16)
        stacked = jnp.concatenate(
            [jnp.where(lane == head, queries, 0.0) for head in range(block_heads)], axis=0
        ).astype(BF16)
        scores = lax.dot_general(
            stacked, keys, (((1,), (1,)), ((), ())), preferred_element_type=F32)
        rows = pl.ds(block * block_heads * length, block_heads * length)
        scores = scores * score_scale + bias_ref[rows, :]
        weights = jnp.exp(scores - jnp.max(scores, axis=1, keepdims=True))
        probs = (weights / jnp.sum(weights, axis=1, keepdims=True)).astype(BF16)
        mixed = jnp.dot(probs, values, preferred_element_type=F32)
        mix = mixed[:length]
        for head in range(1, block_heads):
            mix = jnp.where(lane == head, mixed[head * length : (head + 1) * length], mix)
        mix_ref[:, lanes] = mix.astype(BF16)


def out_part_kernel(masks, *refs):
    peer_refs, rest = grouped(refs, [1] * len(masks))
    own_ref, held_out, stream_ref, total_ref = rest
    total_ref[...] = add_mixes(stream_ref[...].astype(F32), [(lax.axis_index("mp"), own_ref[...])]
                               + peer_blocks(masks, peer_refs), held_out)


def add_mixes(total, blocks, held_out):
    for peer, block in blocks:
        part = held_out[rows_of(peer, block.shape[1]), :]
        total += jnp.dot(block, part, preferred_element_type=F32)
    return total


def out_kernel(masks, keep_section, *refs):
    peer_refs, rest = grouped(refs, [1] * len(masks))
    held_out, partial_ref, kept_ref, result_ref = rest
    total = add_mixes(partial_ref[...], peer_blocks(masks, peer_refs), held_out)
    result = total.astype(BF16)
    if keep_section is not None:
        result = jnp.where(lax.axis_index("section") == keep_section, kept_ref[...], result)
    result_ref[...] = result


def send_kernel(masks, *refs):
    peer_refs, rest = grouped(refs, [1] * len(masks))
    held_out, partial_ref, own_ref, far_ref, to_own_ref, to_far_ref = rest
    total = add_mixes(partial_ref[...], peer_blocks(masks, peer_refs), held_out)
    result = total.astype(BF16)
    last = lax.axis_index("section") == lax.axis_size("section") - 1
    to_own_ref[...] = jnp.where(last, own_ref[...], result)
    to_far_ref[...] = jnp.where(last, far_ref[...], result)


def pick_kernel(section, a_ref, b_ref, o_ref):
    o_ref[...] = jnp.where(lax.axis_index("section") == section, a_ref[...], b_ref[...])


def pick(section, a, b):
    return call(lambda *refs: pick_kernel(section, *refs), [VMEM(a.shape, a.dtype)], a, b)[0]


def shards(micro_inputs, qkv_weight, out_weight, norm_gain, position_bias):
    sections = lax.axis_size("section")
    peers = lax.axis_size("mp")
    length = micro_inputs.shape[1]
    model_width = qkv_weight.shape[1]
    local_heads, bucket_count = position_bias.shape
    local_qkv = qkv_weight.shape[3]
    head_size = local_qkv // local_heads
    weights_qkv = jnp.transpose(qkv_weight[0], (1, 0, 2))
    weights_out = out_weight[0]
    bucket_grid = jnp.asarray(bucket_table(length, bucket_count, REACH))

    total = VMEM((3, length, local_qkv), F32)
    squares = VMEM((length, LANES), F32)
    raw = micro_inputs[0]

    def stay(x):
        return pltpu.with_memory_space_constraint(x, pltpu.HBM)

    def load():
        vm = pl.BlockSpec(memory_space=VMEM)
        hbm = pl.BlockSpec(memory_space=pltpu.HBM)
        sm = pl.BlockSpec(memory_space=pltpu.SMEM)
        return call(
            load_kernel,
            [
                VMEM(raw.shape, BF16), VMEM(norm_gain.shape, BF16),
                VMEM(weights_qkv.shape, BF16),
                total, squares, VMEM((local_heads * length, length), F32),
            ],
            stay(raw), stay(norm_gain), stay(weights_qkv),
            position_bias, stay(bucket_grid),
            specs=[hbm, hbm, hbm, sm, hbm],
            scratch=[VMEM((length, length), jnp.int32), pltpu.SemaphoreType.DMA((peers + 3,))],
        )

    def fetch(x):
        return call(
            fetch_kernel, [VMEM(x.shape, x.dtype)], stay(x),
            specs=[pl.BlockSpec(memory_space=pltpu.HBM)],
            scratch=[pltpu.SemaphoreType.DMA((peers,))],
        )[0]

    def add_own(blocks):
        stream, *parts = call(
            own_kernel, [VMEM(raw.shape, BF16), total, squares], *blocks, gain, held_qkv)
        return stream, parts

    def attend(others, parts):
        for mask, blocks in others[:-1]:
            parts = call(
                lambda *refs, m=mask, n=len(blocks): add_kernel([m], [n], *refs),
                [total, squares], *blocks, gain, held_qkv, *parts)
        late = others[-1:]
        masks = [mask for mask, blocks in late]
        sizes = [len(blocks) for mask, blocks in late]
        return call(
            lambda *refs: attend_kernel(masks, sizes, head_size, model_width, *refs),
            [VMEM((length, local_qkv), BF16)],
            *[x for mask, blocks in late for x in blocks], gain, held_qkv, *parts, bias,
            scratch=[total],
        )[0]

    def project(mixes, mix, stream, keep_section=None, kept=None):
        early, late = mixes[:-2], mixes[-2:]
        early_masks = [mask for mask, blocks in early]
        late_masks = [mask for mask, blocks in late]
        partial = call(
            lambda *refs: out_part_kernel(early_masks, *refs),
            [VMEM(stream.shape, F32)],
            *[blocks[0] for mask, blocks in early], mix, held_out, stream,
        )[0]
        if isinstance(kept, tuple):
            return call(
                lambda *refs: send_kernel(late_masks, *refs),
                [VMEM(stream.shape, BF16)] * 2,
                *[blocks[0] for mask, blocks in late], held_out, partial, *kept,
            )
        return call(
            lambda *refs: out_kernel(late_masks, keep_section, *refs),
            [VMEM(stream.shape, BF16)],
            *[blocks[0] for mask, blocks in late], held_out, partial, stream if kept is None else kept,
        )[0]

    def layer(stream, others, parts, keep_section=None, kept=None, section=None):
        mix = attend(others, parts)
        mixes = from_peers(mix, section=section)
        return project(mixes, mix, stream, keep_section, kept)

    def handed_on(out, far):
        own = crossed(out, 0, 0)
        others = [(FAR, (crossed(far, FAR, 0),))]
        others += [(mask, (swapped(own, mask, 1),)) for mask in REST_ORDER]
        return own, others

    def rotated(x, by):
        return lax.ppermute(x, "section", [(i, (i + by) % sections) for i in range(sections)])

    if sections == 2 and peers == MOST_DIRECT:
        others = [
            (mask, (swapped(raw, mask, 0 if mask in (3,) else None),))
            for mask in FIRST_ORDER
        ]
        ahead = crossed(raw, 3, 1)
        stream, gain, held_qkv, *parts, bias = load()
        held_out = fetch(weights_out)
        far = dict(others)[FAR][0]
        out, far = layer(stream, others, parts, None, (stream, far))
        stream, others = handed_on(out, far)
        others = [(mask, (ahead, *blocks) if mask == 3 else blocks) for mask, blocks in others]
        stream, parts = add_own((stream,))
        out = layer(stream, others, parts)
        finished, others = handed_on(out, out)
        stream, parts = add_own((finished,))
        return layer(stream, others, parts, 0, finished)[None]
    others = from_peers(raw, FIRST_ORDER)
    current, gain, held_qkv, *parts, bias = load()
    held_out = fetch(weights_out)
    ticks = 2 * sections - 1
    result = current
    for tick in range(ticks):
        if tick + 1 < sections:
            raw = rotated(raw, -1)
        out = layer(current, others, parts)
        done = tick - (sections - 1)
        if tick + 1 < ticks:
            sent = rotated(out, 1)
            current = pick(0, raw, sent)
            others = from_peers(current)
            current, parts = add_own((current,))
        if done >= 0:
            owned = rotated(out, done + 1) if done + 1 < sections else out
            result = pick(done, owned, result)
    return result[None]


def solution(mesh):
    in_specs = (
        P(("dp", "section"), None, "mp"),
        P("section", None, None, "mp"),
        P("section", None, "mp"),
        P("section", None),
        P("mp", None),
    )
    out_specs = P(("dp", "section"), None, "mp")
    return jax.shard_map(shards, mesh=mesh, in_specs=in_specs, out_specs=out_specs, check_vma=False)
```

profile of v0, /device:TPU:6, one launch (start us, length us, event | category | flops | bytes accessed | tf_op | source)
XLA Modules:
  0.0 72.5 jit_solution(3900781379003863306)
XLA Ops:
  0.0 1.6 %collective-permute-start.2 = (bf16[64,1024]{1,0:T(8,128)(2,1)}, bf16[64,1024]{1,0:T(8,128)(2,1)S(1)}, u32[]{:S(2)}, u32[]{:S(2)}) collective-permute-start(bf16[64,1024]{1,0:T(8,128)(2,1)} %bitcast.9), channel_id=1, source_target_pairs={{0,3},{1,2},{2,1},{3,0},{4,5},{5,4},{6,7},{7,6},{8,11},{9,10},{10,... | collective-permute-start | bytes 393224 | tf_op jit(solution)/shard_map/ppermute | solution.py:53
  2.0 2.6 %collective-permute-start = (bf16[64,1024]{1,0:T(8,128)(2,1)}, bf16[64,1024]{1,0:T(8,128)(2,1)S(1)}, u32[]{:S(2)}, u32[]{:S(2)}) collective-permute-start(bf16[64,1024]{1,0:T(8,128)(2,1)} %bitcast.11), channel_id=1, source_target_pairs={{0,2},{1,3},{2,0},{3,1},{4,6},{5,7},{6,4},{7,5},{8,10},{9,11},{10,... | collective-permute-start | bytes 393224 | tf_op jit(solution)/shard_map/ppermute | solution.py:53
  5.3 5.4 %shard_map.64 = (bf16[64,1024]{1,0:T(8,128)(2,1)S(1)}, bf16[1,4096]{1,0:T(2,128)(2,1)S(1)}, bf16[3,4096,512]{2,1,0:T(8,128)(2,1)S(1)}, f32[3,64,512]{2,1,0:T(8,1...) custom-call(bf16[64,1024]{1,0:T(8,128)(2,1)} %bitcast.12, bf16[1,4096]{1,0:T(2,128)(2,1)} %gain_in.1, ...), custom_call_target="tpu_custom_call" | custom-call | tf_op jit(solution)/shard_map/pallas_call | solution.py:108
  13.2 1.5 %collective-permute-start.5 = (bf16[64,512]{1,0:T(8,128)(2,1)S(1)}, bf16[64,512]{1,0:T(8,128)(2,1)S(1)}, u32[]{:S(2)}, u32[]{:S(2)}) collective-permute-start(bf16[64,512]{1,0:T(8,128)(2,1)S(1)} %shard_map.67.refs_1_), channel_id=1, source_target_pairs={{0,2},{1,3},{2,0},{3,1},{4,6},{5,7},{6,4},{7,5},{8,10},{9,11},{10,... | collective-permute-start | bytes 196616 | tf_op jit(solution)/shard_map/ppermute | solution.py:53
  14.7 2.5 %collective-permute-start.3 = (bf16[64,512]{1,0:T(8,128)(2,1)S(1)}, bf16[64,512]{1,0:T(8,128)(2,1)S(1)}, u32[]{:S(2)}, u32[]{:S(2)}) collective-permute-start(bf16[64,512]{1,0:T(8,128)(2,1)S(1)} %shard_map.67.refs_1_), channel_id=1, source_target_pairs={{0,3},{1,2},{2,1},{3,0},{4,7},{5,6},{6,5},{7,4},{8,11},{9,10},{10,... | collective-permute-start | bytes 196616 | tf_op jit(solution)/shard_map/ppermute | solution.py:53
  17.2 2.2 %shard_map.68.refs_2_ = bf16[2048,1024]{1,0:T(8,128)(2,1)S(1)} custom-call(bf16[2048,1024]{1,0:T(8,128)(2,1)} %bitcast.8), custom_call_target="tpu_custom_call" | custom-call | tf_op jit(solution)/shard_map/pallas_call | solution.py:108
  19.4 1.8 %collective-permute-done.5.refs_0_ = bf16[64,512]{1,0:T(8,128)(2,1)S(1)} collective-permute-done((bf16[64,512]{1,0:T(8,128)(2,1)S(1)}, bf16[64,512]{1,0:T(8,128)(2,1)S(1)}, u32[]{:S(2)}, u32[]{:S(2)}) %collective-permute-start.5) | collective-permute-done | bytes 65568 | tf_op jit(solution)/shard_map/ppermute | solution.py:53
  22.2 2.4 %collective-permute-start.6 = (bf16[64,1024]{1,0:T(8,128)(2,1)S(1)}, bf16[64,1024]{1,0:T(8,128)(2,1)S(1)}, u32[]{:S(2)}, u32[]{:S(2)}) collective-permute-start(bf16[64,1024]{1,0:T(8,128)(2,1)S(1)} %get-tuple-element.41), channel_id=1, source_target_pairs={{0,4},{1,5},{2,6},{3,7},{4,0},{5,1},{6,2},{7,3},{8,12},{9,13},{10,... | collective-permute-start | bytes 393224 | tf_op jit(solution)/shard_map/ppermute | solution.py:53
  24.7 3.8 %collective-permute-start.8 = (bf16[64,1024]{1,0:T(8,128)(2,1)S(1)}, bf16[64,1024]{1,0:T(8,128)(2,1)S(1)}, u32[]{:S(2)}, u32[]{:S(2)}) collective-permute-start(bf16[64,1024]{1,0:T(8,128)(2,1)S(1)} %bitcast.13), channel_id=1, source_target_pairs={{0,4},{1,5},{2,6},{3,7},{4,3},{5,2},{6,1},{7,0},{8,12},{9,13},{10,... | collective-permute-start | bytes 393224 | tf_op jit(solution)/shard_map/ppermute | solution.py:53
  28.5 1.1 %collective-permute-done.6.refs_0_ = bf16[64,1024]{1,0:T(8,128)(2,1)S(1)} collective-permute-done((bf16[64,1024]{1,0:T(8,128)(2,1)S(1)}, bf16[64,1024]{1,0:T(8,128)(2,1)S(1)}, u32[]{:S(2)}, u32[]{:S(2)}) %collective-permute-start.6) | collective-permute-done | bytes 131104 | tf_op jit(solution)/shard_map/ppermute | solution.py:53
  29.5 2.0 %collective-permute-start.9 = (bf16[64,1024]{1,0:T(8,128)(2,1)S(1)}, bf16[64,1024]{1,0:T(8,128)(2,1)S(1)}, u32[]{:S(2)}, u32[]{:S(2)}) collective-permute-start(bf16[64,1024]{1,0:T(8,128)(2,1)S(1)} %collective-permute-done.6.refs_0_), channel_id=1, source_target_pairs={{0,1},{1,0},{2,3},{3,2},{4,7},{5,6},{6,5},{7,4},{8,9},{9,8},{10,11... | collective-permute-start | bytes 393224 | tf_op jit(solution)/shard_map/ppermute | solution.py:53
  33.5 3.0 %collective-permute-done.9.refs_1_ = bf16[64,1024]{1,0:T(8,128)(2,1)S(1)} collective-permute-done((bf16[64,1024]{1,0:T(8,128)(2,1)S(1)}, bf16[64,1024]{1,0:T(8,128)(2,1)S(1)}, u32[]{:S(2)}, u32[]{:S(2)}) %collective-permute-start.9) | collective-permute-done | bytes 131104 | tf_op jit(solution)/shard_map/ppermute | solution.py:53
  38.9 2.2 %collective-permute-start.13 = (bf16[64,512]{1,0:T(8,128)(2,1)S(1)}, bf16[64,512]{1,0:T(8,128)(2,1)S(1)}, u32[]{:S(2)}, u32[]{:S(2)}) collective-permute-start(bf16[64,512]{1,0:T(8,128)(2,1)S(1)} %shard_map.74.refs_1_), channel_id=1, source_target_pairs={{0,2},{1,3},{2,0},{3,1},{4,6},{5,7},{6,4},{7,5},{8,10},{9,11},{10,... | collective-permute-start | bytes 196616 | tf_op jit(solution)/shard_map/ppermute | solution.py:53
  41.0 1.8 %collective-permute-start.11 = (bf16[64,512]{1,0:T(8,128)(2,1)S(1)}, bf16[64,512]{1,0:T(8,128)(2,1)S(1)}, u32[]{:S(2)}, u32[]{:S(2)}) collective-permute-start(bf16[64,512]{1,0:T(8,128)(2,1)S(1)} %shard_map.74.refs_1_), channel_id=1, source_target_pairs={{0,3},{1,2},{2,1},{3,0},{4,7},{5,6},{6,5},{7,4},{8,11},{9,10},{10,... | collective-permute-start | bytes 196616 | tf_op jit(solution)/shard_map/ppermute | solution.py:53
  42.8 2.3 %collective-permute-done.13.refs_0_ = bf16[64,512]{1,0:T(8,128)(2,1)S(1)} collective-permute-done((bf16[64,512]{1,0:T(8,128)(2,1)S(1)}, bf16[64,512]{1,0:T(8,128)(2,1)S(1)}, u32[]{:S(2)}, u32[]{:S(2)}) %collective-permute-start.13) | collective-permute-done | bytes 65568 | tf_op jit(solution)/shard_map/ppermute | solution.py:53
  45.6 1.5 %collective-permute-done.11.refs_0_ = bf16[64,512]{1,0:T(8,128)(2,1)S(1)} collective-permute-done((bf16[64,512]{1,0:T(8,128)(2,1)S(1)}, bf16[64,512]{1,0:T(8,128)(2,1)S(1)}, u32[]{:S(2)}, u32[]{:S(2)}) %collective-permute-start.11) | collective-permute-done | bytes 65568 | tf_op jit(solution)/shard_map/ppermute | solution.py:53
  48.4 2.0 %collective-permute-start.17 = (bf16[64,1024]{1,0:T(8,128)(2,1)S(1)}, bf16[64,1024]{1,0:T(8,128)(2,1)S(1)}, u32[]{:S(2)}, u32[]{:S(2)}) collective-permute-start(bf16[64,1024]{1,0:T(8,128)(2,1)S(1)} %shard_map.76), channel_id=1, source_target_pairs={{0,6},{1,7},{2,4},{3,5},{4,0},{5,1},{6,2},{7,3},{8,14},{9,15},{10,... | collective-permute-start | bytes 393224 | tf_op jit(solution)/shard_map/ppermute | solution.py:53
  50.3 3.1 %collective-permute-done.14.refs_0_.refs_4_ = bf16[64,1024]{1,0:T(8,128)(2,1)S(1)} collective-permute-done((bf16[64,1024]{1,0:T(8,128)(2,1)S(1)}, bf16[64,1024]{1,0:T(8,128)(2,1)S(1)}, u32[]{:S(2)}, u32[]{:S(2)}) %collective-permute-start.14) | collective-permute-done | bytes 131104 | tf_op jit(solution)/shard_map/ppermute | solution.py:53
  53.5 2.2 %collective-permute-start.16 = (bf16[64,1024]{1,0:T(8,128)(2,1)S(1)}, bf16[64,1024]{1,0:T(8,128)(2,1)S(1)}, u32[]{:S(2)}, u32[]{:S(2)}) collective-permute-start(bf16[64,1024]{1,0:T(8,128)(2,1)S(1)} %collective-permute-done.14.refs_0_.refs_4_), channel_id=1, source_target_pairs={{0,1},{1,0},{2,3},{3,2},{4,7},{5,6},{6,5},{7,4},{8,9},{9,8},{10,11... | collective-permute-start | bytes 393224 | tf_op jit(solution)/shard_map/ppermute | solution.py:53
  57.1 3.3 %collective-permute-done.16.refs_0_ = bf16[64,1024]{1,0:T(8,128)(2,1)S(1)} collective-permute-done((bf16[64,1024]{1,0:T(8,128)(2,1)S(1)}, bf16[64,1024]{1,0:T(8,128)(2,1)S(1)}, u32[]{:S(2)}, u32[]{:S(2)}) %collective-permute-start.16) | collective-permute-done | bytes 131104 | tf_op jit(solution)/shard_map/ppermute | solution.py:53
  61.0 2.4 %collective-permute-done.15.refs_0_ = bf16[64,1024]{1,0:T(8,128)(2,1)S(1)} collective-permute-done((bf16[64,1024]{1,0:T(8,128)(2,1)S(1)}, bf16[64,1024]{1,0:T(8,128)(2,1)S(1)}, u32[]{:S(2)}, u32[]{:S(2)}) %collective-permute-start.15) | collective-permute-done | bytes 131104 | tf_op jit(solution)/shard_map/ppermute | solution.py:53
  64.5 2.2 %collective-permute-start.18 = (bf16[64,512]{1,0:T(8,128)(2,1)S(1)}, bf16[64,512]{1,0:T(8,128)(2,1)S(1)}, u32[]{:S(2)}, u32[]{:S(2)}) collective-permute-start(bf16[64,512]{1,0:T(8,128)(2,1)S(1)} %shard_map.80.refs_1_), channel_id=1, source_target_pairs={{0,3},{1,2},{2,1},{3,0},{4,7},{5,6},{6,5},{7,4},{8,11},{9,10},{10,... | collective-permute-start | bytes 196616 | tf_op jit(solution)/shard_map/ppermute | solution.py:53
  66.7 1.3 %collective-permute-start.19 = (bf16[64,512]{1,0:T(8,128)(2,1)S(1)}, bf16[64,512]{1,0:T(8,128)(2,1)S(1)}, u32[]{:S(2)}, u32[]{:S(2)}) collective-permute-start(bf16[64,512]{1,0:T(8,128)(2,1)S(1)} %shard_map.80.refs_1_), channel_id=1, source_target_pairs={{0,1},{1,0},{2,3},{3,2},{4,5},{5,4},{6,7},{7,6},{8,9},{9,8},{10,11... | collective-permute-start | bytes 196616 | tf_op jit(solution)/shard_map/ppermute | solution.py:53
  68.0 1.7 %collective-permute-done.20.refs_0_ = bf16[64,512]{1,0:T(8,128)(2,1)S(1)} collective-permute-done((bf16[64,512]{1,0:T(8,128)(2,1)S(1)}, bf16[64,512]{1,0:T(8,128)(2,1)S(1)}, u32[]{:S(2)}, u32[]{:S(2)}) %collective-permute-start.20) | collective-permute-done | bytes 65568 | tf_op jit(solution)/shard_map/ppermute | solution.py:53
  (42 shorter events, 16.5 us)
Async XLA Ops:
  0.0 10.7 %collective-permute-start.2 = (bf16[64,1024]{1,0:T(8,128)(2,1)}, bf16[64,1024]{1,0:T(8,128)(2,1)S(1)}, u32[]{:S(2)}, u32[]{:S(2)}) collective-permute-start(bf16[64,1024]{1,0:T(8,128)(2,1)} %bitcast.9), channel_id=1, source_target_pairs={{0,3},{1,2},{2,1},{3,0},{4,5},{5,4},{6,7},{7,6},{8,11},{9,10},{10,... | collective-permute-start | bytes 393224 | tf_op jit(solution)/shard_map/ppermute | solution.py:53
  1.6 9.8 %collective-permute-start.1 = (bf16[64,1024]{1,0:T(8,128)(2,1)}, bf16[64,1024]{1,0:T(8,128)(2,1)S(1)}, u32[]{:S(2)}, u32[]{:S(2)}) collective-permute-start(bf16[64,1024]{1,0:T(8,128)(2,1)} %bitcast.10), channel_id=1, source_target_pairs={{0,1},{1,0},{2,3},{3,2},{4,5},{5,4},{6,7},{7,6},{8,9},{9,8},{10,11... | collective-permute-start | bytes 393224 | tf_op jit(solution)/shard_map/ppermute | solution.py:53
  2.0 10.1 %collective-permute-start = (bf16[64,1024]{1,0:T(8,128)(2,1)}, bf16[64,1024]{1,0:T(8,128)(2,1)S(1)}, u32[]{:S(2)}, u32[]{:S(2)}) collective-permute-start(bf16[64,1024]{1,0:T(8,128)(2,1)} %bitcast.11), channel_id=1, source_target_pairs={{0,2},{1,3},{2,0},{3,1},{4,6},{5,7},{6,4},{7,5},{8,10},{9,11},{10,... | collective-permute-start | bytes 393224 | tf_op jit(solution)/shard_map/ppermute | solution.py:53
  4.6 0.7 copy-start
  12.1 12.6 %copy-start.1 = (bf16[1,64,1024]{2,1,0:T(8,128)(2,1)S(1)}, bf16[1,64,1024]{2,1,0:T(8,128)(2,1)}, u32[]{:S(2)}) copy-start(bf16[1,64,1024]{2,1,0:T(8,128)(2,1)} %param.6) | copy-start | bytes 393220
  13.2 7.9 %collective-permute-start.5 = (bf16[64,512]{1,0:T(8,128)(2,1)S(1)}, bf16[64,512]{1,0:T(8,128)(2,1)S(1)}, u32[]{:S(2)}, u32[]{:S(2)}) collective-permute-start(bf16[64,512]{1,0:T(8,128)(2,1)S(1)} %shard_map.67.refs_1_), channel_id=1, source_target_pairs={{0,2},{1,3},{2,0},{3,1},{4,6},{5,7},{6,4},{7,5},{8,10},{9,11},{10,... | collective-permute-start | bytes 196616 | tf_op jit(solution)/shard_map/ppermute | solution.py:53
  14.7 6.9 %collective-permute-start.3 = (bf16[64,512]{1,0:T(8,128)(2,1)S(1)}, bf16[64,512]{1,0:T(8,128)(2,1)S(1)}, u32[]{:S(2)}, u32[]{:S(2)}) collective-permute-start(bf16[64,512]{1,0:T(8,128)(2,1)S(1)} %shard_map.67.refs_1_), channel_id=1, source_target_pairs={{0,3},{1,2},{2,1},{3,0},{4,7},{5,6},{6,5},{7,4},{8,11},{9,10},{10,... | collective-permute-start | bytes 196616 | tf_op jit(solution)/shard_map/ppermute | solution.py:53
  17.2 4.5 %collective-permute-start.4 = (bf16[64,512]{1,0:T(8,128)(2,1)S(1)}, bf16[64,512]{1,0:T(8,128)(2,1)S(1)}, u32[]{:S(2)}, u32[]{:S(2)}) collective-permute-start(bf16[64,512]{1,0:T(8,128)(2,1)S(1)} %shard_map.67.refs_1_), channel_id=1, source_target_pairs={{0,1},{1,0},{2,3},{3,2},{4,5},{5,4},{6,7},{7,6},{8,9},{9,8},{10,11... | collective-permute-start | bytes 196616 | tf_op jit(solution)/shard_map/ppermute | solution.py:53
  22.2 7.4 %collective-permute-start.6 = (bf16[64,1024]{1,0:T(8,128)(2,1)S(1)}, bf16[64,1024]{1,0:T(8,128)(2,1)S(1)}, u32[]{:S(2)}, u32[]{:S(2)}) collective-permute-start(bf16[64,1024]{1,0:T(8,128)(2,1)S(1)} %get-tuple-element.41), channel_id=1, source_target_pairs={{0,4},{1,5},{2,6},{3,7},{4,0},{5,1},{6,2},{7,3},{8,12},{9,13},{10,... | collective-permute-start | bytes 393224 | tf_op jit(solution)/shard_map/ppermute | solution.py:53
  24.6 8.2 %collective-permute-start.10 = (bf16[64,1024]{1,0:T(8,128)(2,1)S(1)}, bf16[64,1024]{1,0:T(8,128)(2,1)S(1)}, u32[]{:S(2)}, u32[]{:S(2)}) collective-permute-start(bf16[64,1024]{1,0:T(8,128)(2,1)S(1)} %get-tuple-element.42), channel_id=1, source_target_pairs={{0,6},{1,7},{2,4},{3,5},{4,0},{5,1},{6,2},{7,3},{8,14},{9,15},{10,... | collective-permute-start | bytes 393224 | tf_op jit(solution)/shard_map/ppermute | solution.py:53
  24.7 8.8 %collective-permute-start.8 = (bf16[64,1024]{1,0:T(8,128)(2,1)S(1)}, bf16[64,1024]{1,0:T(8,128)(2,1)S(1)}, u32[]{:S(2)}, u32[]{:S(2)}) collective-permute-start(bf16[64,1024]{1,0:T(8,128)(2,1)S(1)} %bitcast.13), channel_id=1, source_target_pairs={{0,4},{1,5},{2,6},{3,7},{4,3},{5,2},{6,1},{7,0},{8,12},{9,13},{10,... | collective-permute-start | bytes 393224 | tf_op jit(solution)/shard_map/ppermute | solution.py:53
  29.5 7.0 %collective-permute-start.9 = (bf16[64,1024]{1,0:T(8,128)(2,1)S(1)}, bf16[64,1024]{1,0:T(8,128)(2,1)S(1)}, u32[]{:S(2)}, u32[]{:S(2)}) collective-permute-start(bf16[64,1024]{1,0:T(8,128)(2,1)S(1)} %collective-permute-done.6.refs_0_), channel_id=1, source_target_pairs={{0,1},{1,0},{2,3},{3,2},{4,7},{5,6},{6,5},{7,4},{8,9},{9,8},{10,11... | collective-permute-start | bytes 393224 | tf_op jit(solution)/shard_map/ppermute | solution.py:53
  31.5 6.3 %collective-permute-start.7 = (bf16[64,1024]{1,0:T(8,128)(2,1)S(1)}, bf16[64,1024]{1,0:T(8,128)(2,1)S(1)}, u32[]{:S(2)}, u32[]{:S(2)}) collective-permute-start(bf16[64,1024]{1,0:T(8,128)(2,1)S(1)} %collective-permute-done.6.refs_0_), channel_id=1, source_target_pairs={{0,1},{1,0},{2,3},{3,2},{4,5},{5,4},{6,7},{7,6},{8,9},{9,8},{10,11... | collective-permute-start | bytes 393224 | tf_op jit(solution)/shard_map/ppermute | solution.py:53
  38.9 6.3 %collective-permute-start.13 = (bf16[64,512]{1,0:T(8,128)(2,1)S(1)}, bf16[64,512]{1,0:T(8,128)(2,1)S(1)}, u32[]{:S(2)}, u32[]{:S(2)}) collective-permute-start(bf16[64,512]{1,0:T(8,128)(2,1)S(1)} %shard_map.74.refs_1_), channel_id=1, source_target_pairs={{0,2},{1,3},{2,0},{3,1},{4,6},{5,7},{6,4},{7,5},{8,10},{9,11},{10,... | collective-permute-start | bytes 196616 | tf_op jit(solution)/shard_map/ppermute | solution.py:53
  41.0 6.1 %collective-permute-start.11 = (bf16[64,512]{1,0:T(8,128)(2,1)S(1)}, bf16[64,512]{1,0:T(8,128)(2,1)S(1)}, u32[]{:S(2)}, u32[]{:S(2)}) collective-permute-start(bf16[64,512]{1,0:T(8,128)(2,1)S(1)} %shard_map.74.refs_1_), channel_id=1, source_target_pairs={{0,3},{1,2},{2,1},{3,0},{4,7},{5,6},{6,5},{7,4},{8,11},{9,10},{10,... | collective-permute-start | bytes 196616 | tf_op jit(solution)/shard_map/ppermute | solution.py:53
  42.8 4.9 %collective-permute-start.12 = (bf16[64,512]{1,0:T(8,128)(2,1)S(1)}, bf16[64,512]{1,0:T(8,128)(2,1)S(1)}, u32[]{:S(2)}, u32[]{:S(2)}) collective-permute-start(bf16[64,512]{1,0:T(8,128)(2,1)S(1)} %shard_map.74.refs_1_), channel_id=1, source_target_pairs={{0,1},{1,0},{2,3},{3,2},{4,5},{5,4},{6,7},{7,6},{8,9},{9,8},{10,11... | collective-permute-start | bytes 196616 | tf_op jit(solution)/shard_map/ppermute | solution.py:53
  48.3 5.2 %collective-permute-start.14 = (bf16[64,1024]{1,0:T(8,128)(2,1)S(1)}, bf16[64,1024]{1,0:T(8,128)(2,1)S(1)}, u32[]{:S(2)}, u32[]{:S(2)}) collective-permute-start(bf16[64,1024]{1,0:T(8,128)(2,1)S(1)} %shard_map.76), channel_id=1, source_target_pairs={{0,4},{1,5},{2,6},{3,7},{4,0},{5,1},{6,2},{7,3},{8,12},{9,13},{10,... | collective-permute-start | bytes 393224 | tf_op jit(solution)/shard_map/ppermute | solution.py:53
  48.4 8.0 %collective-permute-start.17 = (bf16[64,1024]{1,0:T(8,128)(2,1)S(1)}, bf16[64,1024]{1,0:T(8,128)(2,1)S(1)}, u32[]{:S(2)}, u32[]{:S(2)}) collective-permute-start(bf16[64,1024]{1,0:T(8,128)(2,1)S(1)} %shard_map.76), channel_id=1, source_target_pairs={{0,6},{1,7},{2,4},{3,5},{4,0},{5,1},{6,2},{7,3},{8,14},{9,15},{10,... | collective-permute-start | bytes 393224 | tf_op jit(solution)/shard_map/ppermute | solution.py:53
  53.5 6.9 %collective-permute-start.16 = (bf16[64,1024]{1,0:T(8,128)(2,1)S(1)}, bf16[64,1024]{1,0:T(8,128)(2,1)S(1)}, u32[]{:S(2)}, u32[]{:S(2)}) collective-permute-start(bf16[64,1024]{1,0:T(8,128)(2,1)S(1)} %collective-permute-done.14.refs_0_.refs_4_), channel_id=1, source_target_pairs={{0,1},{1,0},{2,3},{3,2},{4,7},{5,6},{6,5},{7,4},{8,9},{9,8},{10,11... | collective-permute-start | bytes 393224 | tf_op jit(solution)/shard_map/ppermute | solution.py:53
  55.7 7.7 %collective-permute-start.15 = (bf16[64,1024]{1,0:T(8,128)(2,1)S(1)}, bf16[64,1024]{1,0:T(8,128)(2,1)S(1)}, u32[]{:S(2)}, u32[]{:S(2)}) collective-permute-start(bf16[64,1024]{1,0:T(8,128)(2,1)S(1)} %collective-permute-done.14.refs_0_.refs_4_), channel_id=1, source_target_pairs={{0,1},{1,0},{2,3},{3,2},{4,5},{5,4},{6,7},{7,6},{8,9},{9,8},{10,11... | collective-permute-start | bytes 393224 | tf_op jit(solution)/shard_map/ppermute | solution.py:53
  64.4 5.2 %collective-permute-start.20 = (bf16[64,512]{1,0:T(8,128)(2,1)S(1)}, bf16[64,512]{1,0:T(8,128)(2,1)S(1)}, u32[]{:S(2)}, u32[]{:S(2)}) collective-permute-start(bf16[64,512]{1,0:T(8,128)(2,1)S(1)} %shard_map.80.refs_1_), channel_id=1, source_target_pairs={{0,2},{1,3},{2,0},{3,1},{4,6},{5,7},{6,4},{7,5},{8,10},{9,11},{10,... | collective-permute-start | bytes 196616 | tf_op jit(solution)/shard_map/ppermute | solution.py:53
  64.5 6.2 %collective-permute-start.18 = (bf16[64,512]{1,0:T(8,128)(2,1)S(1)}, bf16[64,512]{1,0:T(8,128)(2,1)S(1)}, u32[]{:S(2)}, u32[]{:S(2)}) collective-permute-start(bf16[64,512]{1,0:T(8,128)(2,1)S(1)} %shard_map.80.refs_1_), channel_id=1, source_target_pairs={{0,3},{1,2},{2,1},{3,0},{4,7},{5,6},{6,5},{7,4},{8,11},{9,10},{10,... | collective-permute-start | bytes 196616 | tf_op jit(solution)/shard_map/ppermute | solution.py:53
  66.7 4.6 %collective-permute-start.19 = (bf16[64,512]{1,0:T(8,128)(2,1)S(1)}, bf16[64,512]{1,0:T(8,128)(2,1)S(1)}, u32[]{:S(2)}, u32[]{:S(2)}) collective-permute-start(bf16[64,512]{1,0:T(8,128)(2,1)S(1)} %shard_map.80.refs_1_), channel_id=1, source_target_pairs={{0,1},{1,0},{2,3},{3,2},{4,5},{5,4},{6,7},{7,6},{8,9},{9,8},{10,11... | collective-permute-start | bytes 196616 | tf_op jit(solution)/shard_map/ppermute | solution.py:53
where the time goes:
time: 72.7 us; the launch traced here: 72.5 us
  starting transfers between devices  28.7 us (39%)
  waiting for transfers between devices  23.2 us (32%)
  Pallas kernels  19 us (26%)
  local copies, waits for them, and re-layouts  1.35 us (2%)
    ppermute x21, starting transfers between devices, permuted(): return lax.ppermute(x, ('section', 'mp'), pairs)  28.7 us
    ppermute x21, waiting for transfers between devices, permuted(): return lax.ppermute(x, ('section', 'mp'), pairs)  23.2 us
    pallas_call x19, Pallas kernels, call(): return run(*args)  19 us
  transfers between devices with their start and end apart: 21, of which 14 were waited for; matrix products, arithmetic and copies ran while one was open for 0% of the time, Pallas kernels for 20%

commit v1 on v0

--- a/solution.py
+++ b/solution.py
@@ -13,10 +13,11 @@
 NORM_EPSILON = 0.1
 MOST_DIRECT = 4
 FIRST_ORDER = (3, 1, 2)
-MIX_ORDER = (2, 3, 1)
+MIX_ORDER = (2, 1, 3)
 REST_ORDER = (3, 1)
 FAR = 2
 LANES = 128
+DIRECT = 2
 F32 = jnp.float32
 BF16 = jnp.bfloat16
 VMEM = pltpu.VMEM
@@ -95,12 +96,12 @@
     return pl.ds(pl.multiple_of(peer * count, count), count)
 
 
-def call(body, outs, *args, specs=None, scratch=(), limit=8):
+def call(body, outs, *args, specs=None, outs_specs=None, scratch=(), limit=8):
     specs = specs or [pl.BlockSpec(memory_space=VMEM)] * len(args)
     run = pl.pallas_call(
         body,
         in_specs=specs,
-        out_specs=tuple(pl.BlockSpec(memory_space=VMEM) for _ in outs),
+        out_specs=tuple(outs_specs or [pl.BlockSpec(memory_space=VMEM) for _ in outs]),
         out_shape=tuple(outs),
         scratch_shapes=list(scratch),
         compiler_params=pltpu.CompilerParams(vmem_limit_bytes=limit << 20),
@@ -253,6 +254,28 @@
     result_ref[...] = result
 
 
+def last_kernel(masks, keep_section, *refs):
+    peer_refs, rest = grouped(refs, [1] * len(masks))
+    held_out, partial_ref, kept_ref, result_out, result_ref, sems = rest
+    blocks = peer_blocks(masks, peer_refs)
+    half = result_ref.shape[2]
+    copies = []
+    for part in range(result_ref.shape[0]):
+        lanes = pl.ds(part * half, half)
+        total = partial_ref[:, lanes]
+        for peer, block in blocks:
+            weights = held_out[rows_of(peer, block.shape[1]), lanes]
+            total += jnp.dot(block, weights, preferred_element_type=F32)
+        result = jnp.where(
+            lax.axis_index("section") == keep_section, kept_ref[:, lanes], total.astype(BF16))
+        result_ref[part] = result
+        copy = pltpu.make_async_copy(result_ref.at[part], result_out.at[:, lanes], sems.at[part])
+        copy.start()
+        copies.append(copy)
+    for copy in copies:
+        copy.wait()
+
+
 def send_kernel(masks, *refs):
     peer_refs, rest = grouped(refs, [1] * len(masks))
     held_out, partial_ref, own_ref, far_ref, to_own_ref, to_far_ref = rest
@@ -343,6 +366,15 @@
             [VMEM(stream.shape, F32)],
             *[blocks[0] for mask, blocks in early], mix, held_out, stream,
         )[0]
+        if keep_section == 0:
+            halves = VMEM((DIRECT, length, stream.shape[1] // DIRECT), BF16)
+            return call(
+                lambda *refs: last_kernel(late_masks, keep_section, *refs),
+                [jax.ShapeDtypeStruct(stream.shape, BF16)],
+                *[blocks[0] for mask, blocks in late], held_out, partial, kept,
+                outs_specs=[pl.BlockSpec(memory_space=pltpu.HBM)],
+                scratch=[halves, pltpu.SemaphoreType.DMA((DIRECT,))],
+            )[0]
         if isinstance(kept, tuple):
             return call(
                 lambda *refs: send_kernel(late_masks, *refs),

time: 72.7 us -> 73.7 us (1.014)
  the two profiles are of different devices: /device:TPU:6 before, /device:TPU:0 now
where the time goes in v1:
time: 73.7 us; the launch traced here: 73.6 us
  starting transfers between devices  27.7 us (38%)
  waiting for transfers between devices  25.4 us (34%)
  Pallas kernels  19.6 us (27%)
    ppermute x21, starting transfers between devices, permuted(): return lax.ppermute(x, ('section', 'mp'), pairs)  27.7 us
    ppermute x21, waiting for transfers between devices, permuted(): return lax.ppermute(x, ('section', 'mp'), pairs)  25.4 us
    pallas_call x19, Pallas kernels, call(): return run(*args)  19.6 us
  transfers between devices with their start and end apart: 21, of which 14 were waited for; matrix products, arithmetic and copies ran while one was open for 0% of the time, Pallas kernels for 20%

profile of v1, /device:TPU:0, one launch (start us, length us, event | category | flops | bytes accessed | tf_op | source)
XLA Modules:
  0.0 73.6 jit_solution(15878754335421867381)
XLA Ops:
  0.0 5.1 %collective-permute-start.2 = (bf16[64,1024]{1,0:T(8,128)(2,1)}, bf16[64,1024]{1,0:T(8,128)(2,1)S(1)}, u32[]{:S(2)}, u32[]{:S(2)}) collective-permute-start(bf16[64,1024]{1,0:T(8,128)(2,1)} %bitcast.8), channel_id=1, source_target_pairs={{0,3},{1,2},{2,1},{3,0},{4,5},{5,4},{6,7},{7,6},{8,11},{9,10},{10,... | collective-permute-start | bytes 393224 | tf_op jit(solution)/shard_map/ppermute | solution.py:54
  6.3 5.4 %shard_map.64 = (bf16[64,1024]{1,0:T(8,128)(2,1)S(1)}, bf16[1,4096]{1,0:T(2,128)(2,1)S(1)}, bf16[3,4096,512]{2,1,0:T(8,128)(2,1)S(1)}, f32[3,64,512]{2,1,0:T(8,1...) custom-call(bf16[64,1024]{1,0:T(8,128)(2,1)} %bitcast.11, bf16[1,4096]{1,0:T(2,128)(2,1)} %gain_in.1, ...), custom_call_target="tpu_custom_call" | custom-call | tf_op jit(solution)/shard_map/pallas_call | solution.py:109
  13.4 3.0 %collective-permute-done.refs_0_.refs_5_ = bf16[64,1024]{1,0:T(8,128)(2,1)S(1)} collective-permute-done((bf16[64,1024]{1,0:T(8,128)(2,1)}, bf16[64,1024]{1,0:T(8,128)(2,1)S(1)}, u32[]{:S(2)}, u32[]{:S(2)}) %collective-permute-start) | collective-permute-done | bytes 131104 | tf_op jit(solution)/shard_map/ppermute | solution.py:54
  16.4 1.1 %shard_map.67.refs_1_ = bf16[64,512]{1,0:T(8,128)(2,1)S(1)} custom-call(bf16[64,1024]{1,0:T(8,128)(2,1)S(1)} %collective-permute-done.refs_0_.refs_5_, bf16[1,4096]{1,0:T(2,128)(2,1)S(1)} %get-tuple-element.31.refs_1_.refs_2_, bf16[3,4096,512]{2,1,0:T(8,128)(2,1)S(1)} %get-tuple-element.32.refs_2_.refs_3_, f32[3,64,512]{2,1,0:T(8,128)S(1)} %get-tuple-element.37.refs_3_, ...), custom_call_target="tpu_custom_call" | custom-call | tf_op jit(solution)/shard_map/pallas_call | solution.py:109
  18.3 2.2 %collective-permute-start.3 = (bf16[64,512]{1,0:T(8,128)(2,1)S(1)}, bf16[64,512]{1,0:T(8,128)(2,1)S(1)}, u32[]{:S(2)}, u32[]{:S(2)}) collective-permute-start(bf16[64,512]{1,0:T(8,128)(2,1)S(1)} %shard_map.67.refs_1_), channel_id=1, source_target_pairs={{0,1},{1,0},{2,3},{3,2},{4,5},{5,4},{6,7},{7,6},{8,9},{9,8},{10,11... | collective-permute-start | bytes 196616 | tf_op jit(solution)/shard_map/ppermute | solution.py:54
  20.5 1.3 %collective-permute-start.4 = (bf16[64,512]{1,0:T(8,128)(2,1)S(1)}, bf16[64,512]{1,0:T(8,128)(2,1)S(1)}, u32[]{:S(2)}, u32[]{:S(2)}) collective-permute-start(bf16[64,512]{1,0:T(8,128)(2,1)S(1)} %shard_map.67.refs_1_), channel_id=1, source_target_pairs={{0,3},{1,2},{2,1},{3,0},{4,7},{5,6},{6,5},{7,4},{8,11},{9,10},{10,... | collective-permute-start | bytes 196616 | tf_op jit(solution)/shard_map/ppermute | solution.py:54
  21.9 2.2 %shard_map.68.refs_2_ = bf16[2048,1024]{1,0:T(8,128)(2,1)S(1)} custom-call(bf16[2048,1024]{1,0:T(8,128)(2,1)} %bitcast.7), custom_call_target="tpu_custom_call" | custom-call | tf_op jit(solution)/shard_map/pallas_call | solution.py:109
  24.6 2.0 %collective-permute-done.4.refs_1_ = bf16[64,512]{1,0:T(8,128)(2,1)S(1)} collective-permute-done((bf16[64,512]{1,0:T(8,128)(2,1)S(1)}, bf16[64,512]{1,0:T(8,128)(2,1)S(1)}, u32[]{:S(2)}, u32[]{:S(2)}) %collective-permute-start.4) | collective-permute-done | bytes 65568 | tf_op jit(solution)/shard_map/ppermute | solution.py:54
  27.6 1.6 %collective-permute-start.8 = (bf16[64,1024]{1,0:T(8,128)(2,1)S(1)}, bf16[64,1024]{1,0:T(8,128)(2,1)S(1)}, u32[]{:S(2)}, u32[]{:S(2)}) collective-permute-start(bf16[64,1024]{1,0:T(8,128)(2,1)S(1)} %bitcast.12), channel_id=1, source_target_pairs={{0,4},{1,5},{2,6},{3,7},{4,3},{5,2},{6,1},{7,0},{8,12},{9,13},{10,... | collective-permute-start | bytes 393224 | tf_op jit(solution)/shard_map/ppermute | solution.py:54
  29.2 3.6 %collective-permute-done.6.refs_0_ = bf16[64,1024]{1,0:T(8,128)(2,1)S(1)} collective-permute-done((bf16[64,1024]{1,0:T(8,128)(2,1)S(1)}, bf16[64,1024]{1,0:T(8,128)(2,1)S(1)}, u32[]{:S(2)}, u32[]{:S(2)}) %collective-permute-start.6) | collective-permute-done | bytes 131104 | tf_op jit(solution)/shard_map/ppermute | solution.py:54
  32.8 2.0 %collective-permute-start.7 = (bf16[64,1024]{1,0:T(8,128)(2,1)S(1)}, bf16[64,1024]{1,0:T(8,128)(2,1)S(1)}, u32[]{:S(2)}, u32[]{:S(2)}) collective-permute-start(bf16[64,1024]{1,0:T(8,128)(2,1)S(1)} %collective-permute-done.6.refs_0_), channel_id=1, source_target_pairs={{0,1},{1,0},{2,3},{3,2},{4,5},{5,4},{6,7},{7,6},{8,9},{9,8},{10,11... | collective-permute-start | bytes 393224 | tf_op jit(solution)/shard_map/ppermute | solution.py:54
  36.2 1.6 %collective-permute-done.9.refs_1_ = bf16[64,1024]{1,0:T(8,128)(2,1)S(1)} collective-permute-done((bf16[64,1024]{1,0:T(8,128)(2,1)S(1)}, bf16[64,1024]{1,0:T(8,128)(2,1)S(1)}, u32[]{:S(2)}, u32[]{:S(2)}) %collective-permute-start.9) | collective-permute-done | bytes 131104 | tf_op jit(solution)/shard_map/ppermute | solution.py:54
  38.4 2.1 %collective-permute-done.7.refs_0_ = bf16[64,1024]{1,0:T(8,128)(2,1)S(1)} collective-permute-done((bf16[64,1024]{1,0:T(8,128)(2,1)S(1)}, bf16[64,1024]{1,0:T(8,128)(2,1)S(1)}, u32[]{:S(2)}, u32[]{:S(2)}) %collective-permute-start.7) | collective-permute-done | bytes 131104 | tf_op jit(solution)/shard_map/ppermute | solution.py:54
  42.3 3.8 %collective-permute-start.12 = (bf16[64,512]{1,0:T(8,128)(2,1)S(1)}, bf16[64,512]{1,0:T(8,128)(2,1)S(1)}, u32[]{:S(2)}, u32[]{:S(2)}) collective-permute-start(bf16[64,512]{1,0:T(8,128)(2,1)S(1)} %shard_map.74.refs_1_), channel_id=1, source_target_pairs={{0,3},{1,2},{2,1},{3,0},{4,7},{5,6},{6,5},{7,4},{8,11},{9,10},{10,... | collective-permute-start | bytes 196616 | tf_op jit(solution)/shard_map/ppermute | solution.py:54
  46.1 1.4 %collective-permute-done.13.refs_0_ = bf16[64,512]{1,0:T(8,128)(2,1)S(1)} collective-permute-done((bf16[64,512]{1,0:T(8,128)(2,1)S(1)}, bf16[64,512]{1,0:T(8,128)(2,1)S(1)}, u32[]{:S(2)}, u32[]{:S(2)}) %collective-permute-start.13) | collective-permute-done | bytes 65568 | tf_op jit(solution)/shard_map/ppermute | solution.py:54
  47.9 1.1 %collective-permute-done.12.refs_1_ = bf16[64,512]{1,0:T(8,128)(2,1)S(1)} collective-permute-done((bf16[64,512]{1,0:T(8,128)(2,1)S(1)}, bf16[64,512]{1,0:T(8,128)(2,1)S(1)}, u32[]{:S(2)}, u32[]{:S(2)}) %collective-permute-start.12) | collective-permute-done | bytes 65568 | tf_op jit(solution)/shard_map/ppermute | solution.py:54
  49.5 1.8 %collective-permute-start.14 = (bf16[64,1024]{1,0:T(8,128)(2,1)S(1)}, bf16[64,1024]{1,0:T(8,128)(2,1)S(1)}, u32[]{:S(2)}, u32[]{:S(2)}) collective-permute-start(bf16[64,1024]{1,0:T(8,128)(2,1)S(1)} %shard_map.76), channel_id=1, source_target_pairs={{0,4},{1,5},{2,6},{3,7},{4,0},{5,1},{6,2},{7,3},{8,12},{9,13},{10,... | collective-permute-start | bytes 393224 | tf_op jit(solution)/shard_map/ppermute | solution.py:54
  52.1 2.5 %collective-permute-done.14.refs_0_.refs_4_ = bf16[64,1024]{1,0:T(8,128)(2,1)S(1)} collective-permute-done((bf16[64,1024]{1,0:T(8,128)(2,1)S(1)}, bf16[64,1024]{1,0:T(8,128)(2,1)S(1)}, u32[]{:S(2)}, u32[]{:S(2)}) %collective-permute-start.14) | collective-permute-done | bytes 131104 | tf_op jit(solution)/shard_map/ppermute | solution.py:54
  54.5 1.1 %collective-permute-start.16 = (bf16[64,1024]{1,0:T(8,128)(2,1)S(1)}, bf16[64,1024]{1,0:T(8,128)(2,1)S(1)}, u32[]{:S(2)}, u32[]{:S(2)}) collective-permute-start(bf16[64,1024]{1,0:T(8,128)(2,1)S(1)} %collective-permute-done.14.refs_0_.refs_4_), channel_id=1, source_target_pairs={{0,1},{1,0},{2,3},{3,2},{4,7},{5,6},{6,5},{7,4},{8,9},{9,8},{10,11... | collective-permute-start | bytes 393224 | tf_op jit(solution)/shard_map/ppermute | solution.py:54
  57.9 1.6 %collective-permute-done.16.refs_0_ = bf16[64,1024]{1,0:T(8,128)(2,1)S(1)} collective-permute-done((bf16[64,1024]{1,0:T(8,128)(2,1)S(1)}, bf16[64,1024]{1,0:T(8,128)(2,1)S(1)}, u32[]{:S(2)}, u32[]{:S(2)}) %collective-permute-start.16) | collective-permute-done | bytes 131104 | tf_op jit(solution)/shard_map/ppermute | solution.py:54
  61.9 2.3 %collective-permute-start.20 = (bf16[64,512]{1,0:T(8,128)(2,1)S(1)}, bf16[64,512]{1,0:T(8,128)(2,1)S(1)}, u32[]{:S(2)}, u32[]{:S(2)}) collective-permute-start(bf16[64,512]{1,0:T(8,128)(2,1)S(1)} %shard_map.80.refs_1_), channel_id=1, source_target_pairs={{0,2},{1,3},{2,0},{3,1},{4,6},{5,7},{6,4},{7,5},{8,10},{9,11},{10,... | collective-permute-start | bytes 196616 | tf_op jit(solution)/shard_map/ppermute | solution.py:54
  64.3 2.1 %collective-permute-start.18 = (bf16[64,512]{1,0:T(8,128)(2,1)S(1)}, bf16[64,512]{1,0:T(8,128)(2,1)S(1)}, u32[]{:S(2)}, u32[]{:S(2)}) collective-permute-start(bf16[64,512]{1,0:T(8,128)(2,1)S(1)} %shard_map.80.refs_1_), channel_id=1, source_target_pairs={{0,1},{1,0},{2,3},{3,2},{4,5},{5,4},{6,7},{7,6},{8,9},{9,8},{10,11... | collective-permute-start | bytes 196616 | tf_op jit(solution)/shard_map/ppermute | solution.py:54
  68.6 3.8 %collective-permute-done.19.refs_1_ = bf16[64,512]{1,0:T(8,128)(2,1)S(1)} collective-permute-done((bf16[64,512]{1,0:T(8,128)(2,1)S(1)}, bf16[64,512]{1,0:T(8,128)(2,1)S(1)}, u32[]{:S(2)}, u32[]{:S(2)}) %collective-permute-start.19) | collective-permute-done | bytes 65568 | tf_op jit(solution)/shard_map/ppermute | solution.py:54
  72.4 1.1 %shard_map.82 = bf16[64,1024]{1,0:T(8,128)(2,1)} custom-call(bf16[64,512]{1,0:T(8,128)(2,1)S(1)} %collective-permute-done.18.refs_0_, bf16[64,512]{1,0:T(8,128)(2,1)S(1)} %collective-permute-done.19.refs_1_, bf16[2048,1024]{1,0:T(8,128)(2,1)S(1)} %shard_map.68.refs_2_, f32[64,1024]{1,0:T(8,128)S(1)} %shard_map.81.refs_3_, ...), custom_call_target="tpu_custom_call" | custom-call | tf_op jit(solution)/shard_map/pallas_call | solution.py:109
  (41 shorter events, 17.7 us)
Async XLA Ops:
  0.0 11.8 %collective-permute-start.2 = (bf16[64,1024]{1,0:T(8,128)(2,1)}, bf16[64,1024]{1,0:T(8,128)(2,1)S(1)}, u32[]{:S(2)}, u32[]{:S(2)}) collective-permute-start(bf16[64,1024]{1,0:T(8,128)(2,1)} %bitcast.8), channel_id=1, source_target_pairs={{0,3},{1,2},{2,1},{3,0},{4,5},{5,4},{6,7},{7,6},{8,11},{9,10},{10,... | collective-permute-start | bytes 393224 | tf_op jit(solution)/shard_map/ppermute | solution.py:54
  5.1 7.6 %collective-permute-start.1 = (bf16[64,1024]{1,0:T(8,128)(2,1)}, bf16[64,1024]{1,0:T(8,128)(2,1)S(1)}, u32[]{:S(2)}, u32[]{:S(2)}) collective-permute-start(bf16[64,1024]{1,0:T(8,128)(2,1)} %bitcast.9), channel_id=1, source_target_pairs={{0,1},{1,0},{2,3},{3,2},{4,5},{5,4},{6,7},{7,6},{8,9},{9,8},{10,11... | collective-permute-start | bytes 393224 | tf_op jit(solution)/shard_map/ppermute | solution.py:54
  5.1 11.3 %collective-permute-start = (bf16[64,1024]{1,0:T(8,128)(2,1)}, bf16[64,1024]{1,0:T(8,128)(2,1)S(1)}, u32[]{:S(2)}, u32[]{:S(2)}) collective-permute-start(bf16[64,1024]{1,0:T(8,128)(2,1)} %bitcast.10), channel_id=1, source_target_pairs={{0,2},{1,3},{2,0},{3,1},{4,6},{5,7},{6,4},{7,5},{8,10},{9,11},{10,... | collective-permute-start | bytes 393224 | tf_op jit(solution)/shard_map/ppermute | solution.py:54
  5.6 0.7 copy-start
  16.4 11.3 %copy-start.1 = (bf16[1,64,1024]{2,1,0:T(8,128)(2,1)S(1)}, bf16[1,64,1024]{2,1,0:T(8,128)(2,1)}, u32[]{:S(2)}) copy-start(bf16[1,64,1024]{2,1,0:T(8,128)(2,1)} %param.6) | copy-start | bytes 393220
  17.4 6.6 %collective-permute-start.5 = (bf16[64,512]{1,0:T(8,128)(2,1)S(1)}, bf16[64,512]{1,0:T(8,128)(2,1)S(1)}, u32[]{:S(2)}, u32[]{:S(2)}) collective-permute-start(bf16[64,512]{1,0:T(8,128)(2,1)S(1)} %shard_map.67.refs_1_), channel_id=1, source_target_pairs={{0,2},{1,3},{2,0},{3,1},{4,6},{5,7},{6,4},{7,5},{8,10},{9,11},{10,... | collective-permute-start | bytes 196616 | tf_op jit(solution)/shard_map/ppermute | solution.py:54
  18.3 6.3 %collective-permute-start.3 = (bf16[64,512]{1,0:T(8,128)(2,1)S(1)}, bf16[64,512]{1,0:T(8,128)(2,1)S(1)}, u32[]{:S(2)}, u32[]{:S(2)}) collective-permute-start(bf16[64,512]{1,0:T(8,128)(2,1)S(1)} %shard_map.67.refs_1_), channel_id=1, source_target_pairs={{0,1},{1,0},{2,3},{3,2},{4,5},{5,4},{6,7},{7,6},{8,9},{9,8},{10,11... | collective-permute-start | bytes 196616 | tf_op jit(solution)/shard_map/ppermute | solution.py:54
  20.5 6.1 %collective-permute-start.4 = (bf16[64,512]{1,0:T(8,128)(2,1)S(1)}, bf16[64,512]{1,0:T(8,128)(2,1)S(1)}, u32[]{:S(2)}, u32[]{:S(2)}) collective-permute-start(bf16[64,512]{1,0:T(8,128)(2,1)S(1)} %shard_map.67.refs_1_), channel_id=1, source_target_pairs={{0,3},{1,2},{2,1},{3,0},{4,7},{5,6},{6,5},{7,4},{8,11},{9,10},{10,... | collective-permute-start | bytes 196616 | tf_op jit(solution)/shard_map/ppermute | solution.py:54
  27.1 5.7 %collective-permute-start.6 = (bf16[64,1024]{1,0:T(8,128)(2,1)S(1)}, bf16[64,1024]{1,0:T(8,128)(2,1)S(1)}, u32[]{:S(2)}, u32[]{:S(2)}) collective-permute-start(bf16[64,1024]{1,0:T(8,128)(2,1)S(1)} %get-tuple-element.41), channel_id=1, source_target_pairs={{0,4},{1,5},{2,6},{3,7},{4,0},{5,1},{6,2},{7,3},{8,12},{9,13},{10,... | collective-permute-start | bytes 393224 | tf_op jit(solution)/shard_map/ppermute | solution.py:54
  27.1 8.3 %collective-permute-start.10 = (bf16[64,1024]{1,0:T(8,128)(2,1)S(1)}, bf16[64,1024]{1,0:T(8,128)(2,1)S(1)}, u32[]{:S(2)}, u32[]{:S(2)}) collective-permute-start(bf16[64,1024]{1,0:T(8,128)(2,1)S(1)} %get-tuple-element.42), channel_id=1, source_target_pairs={{0,6},{1,7},{2,4},{3,5},{4,0},{5,1},{6,2},{7,3},{8,14},{9,15},{10,... | collective-permute-start | bytes 393224 | tf_op jit(solution)/shard_map/ppermute | solution.py:54
  27.6 8.5 %collective-permute-start.8 = (bf16[64,1024]{1,0:T(8,128)(2,1)S(1)}, bf16[64,1024]{1,0:T(8,128)(2,1)S(1)}, u32[]{:S(2)}, u32[]{:S(2)}) collective-permute-start(bf16[64,1024]{1,0:T(8,128)(2,1)S(1)} %bitcast.12), channel_id=1, source_target_pairs={{0,4},{1,5},{2,6},{3,7},{4,3},{5,2},{6,1},{7,0},{8,12},{9,13},{10,... | collective-permute-start | bytes 393224 | tf_op jit(solution)/shard_map/ppermute | solution.py:54
  32.8 5.0 %collective-permute-start.9 = (bf16[64,1024]{1,0:T(8,128)(2,1)S(1)}, bf16[64,1024]{1,0:T(8,128)(2,1)S(1)}, u32[]{:S(2)}, u32[]{:S(2)}) collective-permute-start(bf16[64,1024]{1,0:T(8,128)(2,1)S(1)} %collective-permute-done.6.refs_0_), channel_id=1, source_target_pairs={{0,1},{1,0},{2,3},{3,2},{4,7},{5,6},{6,5},{7,4},{8,9},{9,8},{10,11... | collective-permute-start | bytes 393224 | tf_op jit(solution)/shard_map/ppermute | solution.py:54
  32.8 7.8 %collective-permute-start.7 = (bf16[64,1024]{1,0:T(8,128)(2,1)S(1)}, bf16[64,1024]{1,0:T(8,128)(2,1)S(1)}, u32[]{:S(2)}, u32[]{:S(2)}) collective-permute-start(bf16[64,1024]{1,0:T(8,128)(2,1)S(1)} %collective-permute-done.6.refs_0_), channel_id=1, source_target_pairs={{0,1},{1,0},{2,3},{3,2},{4,5},{5,4},{6,7},{7,6},{8,9},{9,8},{10,11... | collective-permute-start | bytes 393224 | tf_op jit(solution)/shard_map/ppermute | solution.py:54
  41.6 5.8 %collective-permute-start.13 = (bf16[64,512]{1,0:T(8,128)(2,1)S(1)}, bf16[64,512]{1,0:T(8,128)(2,1)S(1)}, u32[]{:S(2)}, u32[]{:S(2)}) collective-permute-start(bf16[64,512]{1,0:T(8,128)(2,1)S(1)} %shard_map.74.refs_1_), channel_id=1, source_target_pairs={{0,2},{1,3},{2,0},{3,1},{4,6},{5,7},{6,4},{7,5},{8,10},{9,11},{10,... | collective-permute-start | bytes 196616 | tf_op jit(solution)/shard_map/ppermute | solution.py:54
  42.2 5.7 %collective-permute-start.11 = (bf16[64,512]{1,0:T(8,128)(2,1)S(1)}, bf16[64,512]{1,0:T(8,128)(2,1)S(1)}, u32[]{:S(2)}, u32[]{:S(2)}) collective-permute-start(bf16[64,512]{1,0:T(8,128)(2,1)S(1)} %shard_map.74.refs_1_), channel_id=1, source_target_pairs={{0,1},{1,0},{2,3},{3,2},{4,5},{5,4},{6,7},{7,6},{8,9},{9,8},{10,11... | collective-permute-start | bytes 196616 | tf_op jit(solution)/shard_map/ppermute | solution.py:54
  42.3 6.7 %collective-permute-start.12 = (bf16[64,512]{1,0:T(8,128)(2,1)S(1)}, bf16[64,512]{1,0:T(8,128)(2,1)S(1)}, u32[]{:S(2)}, u32[]{:S(2)}) collective-permute-start(bf16[64,512]{1,0:T(8,128)(2,1)S(1)} %shard_map.74.refs_1_), channel_id=1, source_target_pairs={{0,3},{1,2},{2,1},{3,0},{4,7},{5,6},{6,5},{7,4},{8,11},{9,10},{10,... | collective-permute-start | bytes 196616 | tf_op jit(solution)/shard_map/ppermute | solution.py:54
  49.5 5.0 %collective-permute-start.14 = (bf16[64,1024]{1,0:T(8,128)(2,1)S(1)}, bf16[64,1024]{1,0:T(8,128)(2,1)S(1)}, u32[]{:S(2)}, u32[]{:S(2)}) collective-permute-start(bf16[64,1024]{1,0:T(8,128)(2,1)S(1)} %shard_map.76), channel_id=1, source_target_pairs={{0,4},{1,5},{2,6},{3,7},{4,0},{5,1},{6,2},{7,3},{8,12},{9,13},{10,... | collective-permute-start | bytes 393224 | tf_op jit(solution)/shard_map/ppermute | solution.py:54
  51.3 5.9 %collective-permute-start.17 = (bf16[64,1024]{1,0:T(8,128)(2,1)S(1)}, bf16[64,1024]{1,0:T(8,128)(2,1)S(1)}, u32[]{:S(2)}, u32[]{:S(2)}) collective-permute-start(bf16[64,1024]{1,0:T(8,128)(2,1)S(1)} %shard_map.76), channel_id=1, source_target_pairs={{0,6},{1,7},{2,4},{3,5},{4,0},{5,1},{6,2},{7,3},{8,14},{9,15},{10,... | collective-permute-start | bytes 393224 | tf_op jit(solution)/shard_map/ppermute | solution.py:54
  54.5 5.0 %collective-permute-start.16 = (bf16[64,1024]{1,0:T(8,128)(2,1)S(1)}, bf16[64,1024]{1,0:T(8,128)(2,1)S(1)}, u32[]{:S(2)}, u32[]{:S(2)}) collective-permute-start(bf16[64,1024]{1,0:T(8,128)(2,1)S(1)} %collective-permute-done.14.refs_0_.refs_4_), channel_id=1, source_target_pairs={{0,1},{1,0},{2,3},{3,2},{4,7},{5,6},{6,5},{7,4},{8,9},{9,8},{10,11... | collective-permute-start | bytes 393224 | tf_op jit(solution)/shard_map/ppermute | solution.py:54
  55.6 5.3 %collective-permute-start.15 = (bf16[64,1024]{1,0:T(8,128)(2,1)S(1)}, bf16[64,1024]{1,0:T(8,128)(2,1)S(1)}, u32[]{:S(2)}, u32[]{:S(2)}) collective-permute-start(bf16[64,1024]{1,0:T(8,128)(2,1)S(1)} %collective-permute-done.14.refs_0_.refs_4_), channel_id=1, source_target_pairs={{0,1},{1,0},{2,3},{3,2},{4,5},{5,4},{6,7},{7,6},{8,9},{9,8},{10,11... | collective-permute-start | bytes 393224 | tf_op jit(solution)/shard_map/ppermute | solution.py:54
  61.9 5.2 %collective-permute-start.20 = (bf16[64,512]{1,0:T(8,128)(2,1)S(1)}, bf16[64,512]{1,0:T(8,128)(2,1)S(1)}, u32[]{:S(2)}, u32[]{:S(2)}) collective-permute-start(bf16[64,512]{1,0:T(8,128)(2,1)S(1)} %shard_map.80.refs_1_), channel_id=1, source_target_pairs={{0,2},{1,3},{2,0},{3,1},{4,6},{5,7},{6,4},{7,5},{8,10},{9,11},{10,... | collective-permute-start | bytes 196616 | tf_op jit(solution)/shard_map/ppermute | solution.py:54
  64.3 4.4 %collective-permute-start.18 = (bf16[64,512]{1,0:T(8,128)(2,1)S(1)}, bf16[64,512]{1,0:T(8,128)(2,1)S(1)}, u32[]{:S(2)}, u32[]{:S(2)}) collective-permute-start(bf16[64,512]{1,0:T(8,128)(2,1)S(1)} %shard_map.80.refs_1_), channel_id=1, source_target_pairs={{0,1},{1,0},{2,3},{3,2},{4,5},{5,4},{6,7},{7,6},{8,9},{9,8},{10,11... | collective-permute-start | bytes 196616 | tf_op jit(solution)/shard_map/ppermute | solution.py:54
  66.4 6.1 %collective-permute-start.19 = (bf16[64,512]{1,0:T(8,128)(2,1)S(1)}, bf16[64,512]{1,0:T(8,128)(2,1)S(1)}, u32[]{:S(2)}, u32[]{:S(2)}) collective-permute-start(bf16[64,512]{1,0:T(8,128)(2,1)S(1)} %shard_map.80.refs_1_), channel_id=1, source_target_pairs={{0,3},{1,2},{2,1},{3,0},{4,7},{5,6},{6,5},{7,4},{8,11},{9,10},{10,... | collective-permute-start | bytes 196616 | tf_op jit(solution)/shard_map/ppermute | solution.py:54
